TPU v7x, 16 devices: a whole 2x2x2 slice. The times are simulated.
16 devices in a mesh: fsdp: 2 (over z), tp: 8 (over y, x, core).
Axes of the slice: x: 2, y: 2, z: 2, core: 2. Of those that a mesh axis runs over, the one named last changes fastest.
Arguments:
- x: bfloat16 [16384, 4096], P(('fsdp', 'tp'))
- gamma: float32 [4096], replicated
- w1: bfloat16 [4096, 16384], P('fsdp', 'tp')
- w2: bfloat16 [16384, 4096], P('tp', 'fsdp')
Outputs:
- output: bfloat16 [16384, 4096], P(('fsdp', 'tp'))
All inputs are finite; a program needn't handle non-finite values.
Results may differ from a plain program's by a relative error of at most 0.001.
Values are sent between devices in bfloat16 or wider.
A program may use at most 1 GiB of HBM per device.

v0:
```python
import jax
import jax.numpy as jnp
from jax import lax
from jax.sharding import PartitionSpec as P

EPS = 1e-6


def _norm(x, gamma):
    xf = x.astype(jnp.float32)
    mu = jnp.mean(xf, axis=-1, keepdims=True)
    var = jnp.mean(jnp.square(xf - mu), axis=-1, keepdims=True)
    return xf, ((xf - mu) * lax.rsqrt(var + EPS) * gamma).astype(jnp.bfloat16)


def solution(mesh):
    def body(x, gamma, w1, w2):
        w1f = lax.all_gather(w1, "fsdp", axis=0, tiled=True)
        w2f = lax.all_gather(w2, "fsdp", axis=1, tiled=True)
        xf, xn = _norm(x, gamma)
        xg = lax.all_gather(xn, "tp", axis=0, tiled=True)
        h = jax.nn.gelu(jnp.dot(xg, w1f, preferred_element_type=jnp.float32), approximate=True).astype(jnp.bfloat16)
        yp = jnp.dot(h, w2f, preferred_element_type=jnp.float32)
        y = lax.psum_scatter(yp, "tp", scatter_dimension=0, tiled=True)
        return (xf + y).astype(jnp.bfloat16)

    return jax.shard_map(
        body,
        mesh=mesh,
        in_specs=(P(("fsdp", "tp"), None), P(None), P("fsdp", "tp"), P("tp", "fsdp")),
        out_specs=P(("fsdp", "tp"), None),
        check_vma=False,
    )
```

profile of v0, /device:TPU:0, one launch (start us, length us, event | category | flops | bytes accessed | tf_op | source)
XLA Modules:
  0.0 1620.6 jit_solution(15379851207027897935)
XLA Ops:
  6.5 0.0 copy-start
  6.5 0.0 all-gather.6.cloned.1.call-start
  6.5 0.7 all-gather.6.cloned.1.call-update
  7.3 0.0 all-gather.4.cloned.1.call-start
  7.3 4.5 convert_reduce_fusion
  11.9 5.7 fusion.16
  17.6 0.0 copy-done
  17.6 11.5 fusion.18
  29.1 0.0 all-gather.4.cloned.1.call-update
  29.1 0.0 all-gather.8.cloned.1.call-start
  29.1 0.7 all-gather.8.cloned.1.call-update
  29.8 0.2 reduce-scatter.2.cloned.1.call-start
  30.1 179.3 %all-gather.6.cloned.1.call-done = bf16[4096,2048]{1,0:T(8,128)(2,1)} async-done(((bf16[2048,2048]{1,0:T(8,128)(2,1)}), bf16[4096,2048]{1,0:T(8,128)(2,1)}) %all-gather.6.cloned.1.call-update) | async-done | bytes 16777232 | tf_op jit(solution)/shard_map/all_gather | solution.py:18
  209.3 300.9 %all-gather.4.cloned.1.call-done = bf16[8192,4096]{1,0:T(8,128)(2,1)} async-done(((bf16[1024,4096]{1,0:T(8,128)(2,1)}), bf16[8192,4096]{1,0:T(8,128)(2,1)}) %all-gather.4.cloned.1.call-update) | async-done | bytes 67108880 | tf_op jit(solution)/shard_map/all_gather | solution.py:21
  510.2 150.9 %fusion.24 = f32[8192,2048]{1,0:T(8,128)} fusion(bf16[8192,4096]{1,0:T(8,128)(2,1)} %all-gather.4.cloned.1.call-done, bf16[4096,2048]{1,0:T(8,128)(2,1)} %all-gather.6.cloned.1.call-done), kind=kOutput, calls=%fused_computation.29 | convolution fusion | flops 137438953472 | bytes 150994944 | tf_op jit(solution)/shard_map/dot_general | solution.py:22
  661.1 48.3 %all-gather.8.cloned.1.call-done = bf16[2048,4096]{1,0:T(8,128)(2,1)} async-done(((bf16[2048,2048]{1,0:T(8,128)(2,1)}), bf16[2048,4096]{1,0:T(8,128)(2,1)}) %all-gather.8.cloned.1.call-update) | async-done | bytes 16777232 | tf_op jit(solution)/shard_map/all_gather | solution.py:19
  709.4 158.0 %fusion.8 = f32[8192,4096]{1,0:T(8,128)} fusion(bf16[2048,4096]{1,0:T(8,128)(2,1)} %all-gather.8.cloned.1.call-done, f32[8192,2048]{1,0:T(8,128)} %fusion.24), kind=kOutput, calls=%fused_computation.9 | convolution fusion | flops 137589948416 | bytes 218103808 | tf_op jit(solution)/shard_map/dot_general | solution.py:23
  867.3 0.0 reduce-scatter.2.cloned.1.call-update
  867.3 734.7 %reduce-scatter.2.cloned.1.call-done = f32[1024,4096]{1,0:T(8,128)} async-done(((f32[8192,4096]{1,0:T(8,128)}), f32[1024,4096]{1,0:T(8,128)}) %reduce-scatter.2.cloned.1.call-update) | async-done | bytes 16777232 | tf_op jit(solution)/shard_map/reduce_scatter | solution.py:24
  1602.0 12.0 fusion.19
  (2 shorter events, 0.0 us)
Async XLA Ops:
  6.5 11.0 copy-start
  6.5 202.8 %all-gather.6.cloned.1.call-start = ((), (), s32[]{:S(2)}) async-start(), calls=%async_computation.2 | async-start | bytes 25165824 | tf_op jit(solution)/shard_map/all_gather | solution.py:18
  7.3 502.9 %all-gather.4.cloned.1.call-start = ((), (), s32[]{:S(2)}) async-start(), calls=%async_computation.1 | async-start | bytes 75497472 | tf_op jit(solution)/shard_map/all_gather | solution.py:21
  29.1 680.3 %all-gather.8.cloned.1.call-start = ((), (), s32[]{:S(2)}) async-start(), calls=%async_computation.3 | async-start | bytes 25165824 | tf_op jit(solution)/shard_map/all_gather | solution.py:19
  29.8 1572.2 %reduce-scatter.2.cloned.1.call-start = ((), (), s32[]{:S(2)}) async-start(), calls=%async_computation.4 | async-start | bytes 150994944 | tf_op jit(solution)/shard_map/reduce_scatter | solution.py:24
Sparse Core Ops, SparseCore 0:
  8.9 200.4 all-gather.5
  211.1 299.0 all-gather.3
  511.7 197.5 all-gather.7
  867.5 734.5 reduce-scatter.1
where the time goes:
time: 1620 us
  waiting for transfers between devices  1260 us (78%)
  matrix products  309 us (19%)
  other arithmetic  33.8 us (2%)
    reduce_scatter x1, waiting for transfers between devices, body(): y = lax.psum_scatter(yp, 'tp', scatter_dimension=0, tiled=True)  735 us
    all_gather x1, waiting for transfers between devices, body(): xg = lax.all_gather(xn, 'tp', axis=0, tiled=True)  301 us
    all_gather x1, waiting for transfers between devices, body(): w1f = lax.all_gather(w1, 'fsdp', axis=0, tiled=True)  179 us
    dot_general x1, matrix products, body(): yp = jnp.dot(h, w2f, preferred_element_type=jnp.float32)  158 us
    dot_general x1, matrix products, body(): jnp.dot(xg, w1f, preferred_element_type=jnp.float32)  151 us
    all_gather x1, waiting for transfers between devices, body(): w2f = lax.all_gather(w2, 'fsdp', axis=1, tiled=True)  48.3 us
  transfers between devices with their start and end apart: 4, of which 4 were waited for; matrix products, arithmetic and copies ran while one was open for 11% of the time, Pallas kernels for 0%

commit v1 on v0

v1 whole, which is shorter than its diff:
```python
import functools

import jax
import jax.numpy as jnp
from jax import lax
from jax.experimental import pallas as pl
from jax.experimental.pallas import tpu as pltpu
from jax.sharding import PartitionSpec as P

EPS = 1e-6
MESH = pl.DeviceIdType.MESH

ROWS, D, HALF = 1024, 4096, 2048
W = 256
NC = HALF // W
NJ = 2 * NC
BM = 512
XR = 256
LAG = 3
Y, Z, DIAG, SIB = 1, 2, 3, 4


def _kernel(x, gamma, w1, w2, y, g1, g2, xnh, xph, rbuf, h, wt, send, recv, xsend, xrecv, psend, precv, loc):
    f, t = lax.axis_index("fsdp"), lax.axis_index("tp")
    core, ix, iy = lax.rem(t, 2), lax.rem(t // 2, 2), t // 4
    to_core, to_x, to_y, to_z = (f, t + 1 - 2 * core), (f, t + 2 - 4 * ix), (f, t + 4 - 8 * iy), (1 - f, t)
    shard, got = (w1, w2), (g1, g2)
    mine, other = pl.multiple_of(f * HALF, HALF), pl.multiple_of((1 - f) * HALF, HALF)

    barrier = pltpu.get_barrier_semaphore()
    for d in (to_core, to_x, to_y, to_z):
        pl.semaphore_signal(barrier, inc=1, device_id=d, device_id_type=MESH)
    pl.semaphore_wait(barrier, 4)

    def cols(c):
        return pl.ds(pl.multiple_of(c * W, W), W)

    def copy(w, kind, src, dst_piece, c, device):
        return pltpu.make_async_remote_copy(
            src_ref=shard[w].at[:, cols(c)] if src == 0 else got[w].at[src, c],
            dst_ref=got[w].at[dst_piece, c],
            send_sem=send.at[w, kind, c],
            recv_sem=recv.at[w, dst_piece - 1, c],
            device_id=device,
            device_id_type=MESH,
        )

    def arrived(w, piece, c):
        at = got[w].at[piece, c]
        pltpu.make_async_copy(at, at, recv.at[w, piece - 1, c]).wait()

    def send_own(w, g):
        for k in range(2):
            copy(w, 0, 0, Y, 2 * g + k, to_y).start()
            copy(w, 1, 0, Z, 2 * g + 1 - k, to_z).start()
            copy(w, 2, 0, SIB, 2 * g + k, to_core).start()

    def to_sib(w, piece, c):
        copy(w, 2 + piece, piece, SIB + piece, c, to_core).start()

    def slot_a(w, g):
        arrived(w, Y, 2 * g)
        arrived(w, Z, 2 * g + 1)
        copy(w, 6, Z, DIAG, 2 * g + 1, to_y).start()
        copy(w, 6, Y, DIAG, 2 * g, to_z).start()
        if w == 0:
            send_own(*((0, g + 1) if g < 3 else (1, 0)))
        else:
            pl.when(g < 3)(lambda: send_own(1, g + 1))
        to_sib(w, Y, 2 * g)
        to_sib(w, Z, 2 * g + 1)

    def slot_b(w, g):
        arrived(w, Y, 2 * g + 1)
        arrived(w, Z, 2 * g)
        to_sib(w, Y, 2 * g + 1)
        to_sib(w, Z, 2 * g)

    def slot_c(w, g):
        arrived(w, DIAG, 2 * g)
        arrived(w, DIAG, 2 * g + 1)
        to_sib(w, DIAG, 2 * g)
        to_sib(w, DIAG, 2 * g + 1)

    send_own(0, 0)

    def x_in(i):
        return pltpu.make_async_copy(x.at[pl.ds(i * XR, XR)], h.at[pl.ds(i * XR, XR), pl.ds(0, D)], loc.at[i])

    def xn_out(i):
        return pltpu.make_async_copy(h.at[pl.ds(i * XR, XR), pl.ds(0, D)], xnh.at[pl.ds(i * XR, XR)], loc.at[4 + i])

    def xn_send(i):
        rows = pl.ds(i * XR, XR)
        return pltpu.make_async_remote_copy(
            src_ref=xnh.at[rows], dst_ref=xph.at[rows], send_sem=xsend.at[i], recv_sem=xrecv.at[i],
            device_id=to_x, device_id_type=MESH,
        )

    nx = ROWS // XR
    for i in range(nx):
        x_in(i).start()
    for i in range(nx):
        x_in(i).wait()

        def norm(b, _, i=i):
            rows = pl.ds(pl.multiple_of(i * XR + b * 16, 16), 16)
            xf = h[rows, pl.ds(0, D)].astype(jnp.float32)
            mu = jnp.mean(xf, axis=-1, keepdims=True)
            xc = xf - mu
            var = jnp.mean(jnp.square(xc), axis=-1, keepdims=True)
            h[rows, pl.ds(0, D)] = (xc * lax.rsqrt(var + EPS) * gamma[...]).astype(jnp.bfloat16)
            return 0

        lax.fori_loop(0, XR // 16, norm, 0)
        xn_out(i).start()
        if i > 0:
            xn_out(i - 1).wait()
            xn_send(i - 1).start()
    xn_out(nx - 1).wait()
    xn_send(nx - 1).start()

    def first(xn):
        def load_tokens(src, row):
            for k, at in enumerate((mine, other)):
                pltpu.make_async_copy(
                    src.at[:, pl.ds(at, HALF)], xn.at[pl.ds(row, ROWS), pl.ds(k * HALF, HALF)], loc.at[k]
                ).start()
            for k, at in enumerate((mine, other)):
                pltpu.make_async_copy(
                    src.at[:, pl.ds(at, HALF)], xn.at[pl.ds(row, ROWS), pl.ds(k * HALF, HALF)], loc.at[k]
                ).wait()

        load_tokens(xnh, 0)

        def tiles(s, c, n, row, rows, new):
            def load(q, k):
                cc, sib = c + q // 2, SIB * (q % 2)
                src = w1.at[:, cols(cc)] if (sib, k, s) == (0, 0, 0) else g1.at[sib + 2 * k + s, cc]
                return pltpu.make_async_copy(src, wt.at[q, pl.ds(k * HALF, HALF)], loc.at[2 * q + k])

            for q in range(2 * n):
                for k in range(2):
                    if new and q % 2:
                        arrived(0, SIB + 2 * k + s, c + q // 2)
                    load(q, k).start()
            nb = rows // BM

            def product(i, _):
                q, b = i // nb, lax.rem(i, nb)
                for qq in range(2 * n):

                    @pl.when(i == qq * nb)
                    def _(qq=qq):
                        for k in range(2):
                            load(qq, k).wait()

                r = pl.ds(pl.multiple_of(row + b * BM, BM), BM)
                pre = jnp.dot(xn[r, :], wt[q], preferred_element_type=jnp.float32)
                at = (lax.rem(q, 2) * 2 + s) * HALF + (c + q // 2) * W
                h[r, pl.ds(pl.multiple_of(at, W), W)] = jax.nn.gelu(pre, approximate=True).astype(jnp.bfloat16)
                return 0

            lax.fori_loop(0, 2 * n * nb, product, 0)

        for g in range(3):
            slot_a(0, g)
            tiles(0, 2 * g + 1, 1, 0, ROWS, True)
            slot_b(0, g)
            tiles(0, 2 * g, 1, 0, ROWS, True)
            if g < 2:
                slot_c(0, g)
                tiles(1, 2 * g, 2, 0, ROWS, True)
        for i in range(nx):
            xn_send(i).wait_recv()
        load_tokens(xph, ROWS)
        for s in range(2):
            tiles(s, 0, 2, ROWS, ROWS, False)
        slot_c(0, 2)
        for s in range(2):
            tiles(s, 2, 2, ROWS, ROWS, False)
        tiles(1, 4, 2, 0, 2 * ROWS, True)
        slot_a(0, 3)
        tiles(0, 4, 2, ROWS, ROWS, False)
        tiles(0, 7, 1, 0, 2 * ROWS, True)
        slot_b(0, 3)
        tiles(0, 6, 1, 0, 2 * ROWS, True)
        slot_c(0, 3)
        tiles(1, 6, 2, 0, 2 * ROWS, True)

    pl.run_scoped(first, pltpu.VMEM((2 * ROWS, D), jnp.bfloat16))

    def second(theirs, own, back, xb, yb):
        def where(j):
            r, c = lax.rem(j, 4) // 2, 2 * (j // 4) + lax.rem(j, 2)
            return r, c, pl.multiple_of(lax.rem(f + r, 2) * HALF + c * W, W)

        def partial_out(j):
            return pltpu.make_async_remote_copy(
                src_ref=theirs.at[lax.rem(j, LAG)], dst_ref=rbuf.at[j], send_sem=psend.at[j], recv_sem=precv.at[j],
                device_id=to_x, device_id_type=MESH,
            )

        def y_out(j):
            _, _, at = where(j)
            return pltpu.make_async_copy(yb.at[lax.rem(j, 2)], y.at[:, pl.ds(at, W)], loc.at[6 + lax.rem(j, 2)])

        def finish(j):
            _, _, at = where(j)
            a = pltpu.make_async_copy(x.at[:, pl.ds(at, W)], xb, loc.at[4])
            b = pltpu.make_async_copy(rbuf.at[j], back, loc.at[5])
            a.start()
            partial_out(j).wait_recv()
            b.start()
            pl.when(j >= 2)(lambda: y_out(j - 2).wait())
            a.wait()
            b.wait()

            def add(i, _):
                r = pl.ds(pl.multiple_of(i * 64, 64), 64)
                total = own[lax.rem(j, LAG + 1), r, :] + back[r, :]
                yb[lax.rem(j, 2), r, :] = (xb[r, :].astype(jnp.float32) + total).astype(jnp.bfloat16)
                return 0

            lax.fori_loop(0, ROWS // 64, add, 0)
            y_out(j).start()

        def product(row, b):
            r = pl.ds(pl.multiple_of(row + b * BM, BM), BM)
            return sum(
                jnp.dot(h[r, pl.ds(k * D, D)], wt[k], preferred_element_type=jnp.float32) for k in range(2)
            )

        def chunk(j, _):
            g, q = j // 4, lax.rem(j, 4)
            r, c, _ = where(j)
            pl.when(q == 0)(lambda: slot_a(1, g))
            pl.when(q == 1)(lambda: slot_b(1, g))
            pl.when(q == 2)(lambda: slot_c(1, g))

            def load(sib, s):
                src = g2.at[SIB * sib + 2 * r + s, c]
                return pltpu.make_async_copy(src, wt.at[sib, pl.ds(s * HALF, HALF)], loc.at[2 * sib + s])

            @pl.when(r == 0)
            def _():
                pltpu.make_async_copy(w2.at[:, cols(c)], wt.at[0, pl.ds(0, HALF)], loc.at[0]).start()

            @pl.when(r == 1)
            def _():
                load(0, 0).start()

            load(0, 1).start()
            for s in range(2):
                arrived(1, SIB + 2 * r + s, c)
                load(1, s).start()
            pl.when(j >= LAG)(lambda: partial_out(j - LAG).wait_send())
            for sib in range(2):
                for s in range(2):
                    load(sib, s).wait()

            def to_them(b, _):
                theirs[lax.rem(j, LAG), pl.ds(pl.multiple_of(b * BM, BM), BM), :] = product(ROWS, b)
                return 0

            lax.fori_loop(0, ROWS // BM, to_them, 0)
            partial_out(j).start()

            def to_us(b, _):
                own[lax.rem(j, LAG + 1), pl.ds(pl.multiple_of(b * BM, BM), BM), :] = product(0, b)
                return 0

            lax.fori_loop(0, ROWS // BM, to_us, 0)
            pl.when(j >= LAG)(lambda: finish(j - LAG))
            return 0

        lax.fori_loop(0, NJ, chunk, 0)

        def drain(j, _):
            finish(j)
            partial_out(j).wait_send()
            return 0

        lax.fori_loop(NJ - LAG, NJ, drain, 0)
        for j in range(NJ - 2, NJ):
            y_out(j).wait()

    pl.run_scoped(
        second,
        pltpu.VMEM((LAG, ROWS, W), jnp.float32),
        pltpu.VMEM((LAG + 1, ROWS, W), jnp.float32),
        pltpu.VMEM((ROWS, W), jnp.float32),
        pltpu.VMEM((ROWS, W), jnp.bfloat16),
        pltpu.VMEM((2, ROWS, W), jnp.bfloat16),
    )

    for i in range(nx):
        xn_send(i).wait_send()

    def sent(c, _):
        for w in range(2):
            for kind in range(7):
                copy(w, kind, Y, Y, c, to_y).wait_send()
        return 0

    lax.fori_loop(0, NC, sent, 0)


def solution(mesh):
    hbm = pl.BlockSpec(memory_space=pltpu.HBM)
    vmem = pl.BlockSpec(memory_space=pltpu.VMEM)

    def body(x, gamma, w1, w2):
        bf16 = functools.partial(jax.ShapeDtypeStruct, dtype=jnp.bfloat16)
        out = pl.pallas_call(
            _kernel,
            out_shape=[
                bf16((ROWS, D)),
                bf16((8, NC, HALF, W)),
                bf16((8, NC, HALF, W)),
                bf16((ROWS, D)),
                bf16((ROWS, D)),
                jax.ShapeDtypeStruct((NJ, ROWS, W), jnp.float32),
            ],
            in_specs=[hbm, vmem, hbm, hbm],
            out_specs=[hbm] * 6,
            scratch_shapes=[
                pltpu.VMEM((2 * ROWS, 4 * HALF), jnp.bfloat16),
                pltpu.VMEM((4, D, W), jnp.bfloat16),
                pltpu.SemaphoreType.DMA((2, 7, NC)),
                pltpu.SemaphoreType.DMA((2, 7, NC)),
                pltpu.SemaphoreType.DMA((ROWS // XR,)),
                pltpu.SemaphoreType.DMA((ROWS // XR,)),
                pltpu.SemaphoreType.DMA((NJ,)),
                pltpu.SemaphoreType.DMA((NJ,)),
                pltpu.SemaphoreType.DMA((8,)),
            ],
            compiler_params=pltpu.CompilerParams(
                collective_id=0, has_side_effects=True, vmem_limit_bytes=67_043_328
            ),
            cost_estimate=pl.CostEstimate(flops=275_000_000_000, bytes_accessed=400_000_000, transcendentals=16_777_216),
        )(x, gamma.reshape(1, D), w1, w2)
        return out[0]

    return jax.shard_map(
        body,
        mesh=mesh,
        in_specs=(P(("fsdp", "tp"), None), P(None), P("fsdp", "tp"), P("tp", "fsdp")),
        out_specs=P(("fsdp", "tp"), None),
        check_vma=False,
    )
```

time: 1620 us -> 718 us (0.44)
  waiting for transfers between devices: 1260 us -> 0 us
  Pallas kernels: 0 us -> 710 us
  matrix products: 309 us -> 0 us
  other arithmetic: 33.8 us -> 0 us
    reduce_scatter x1 -> x0, waiting for transfers between devices: 735 us -> none  [body(): y = lax.psum_scatter(yp, 'tp', scatter_dimension=0, tiled=True)]
    pallas_call x0 -> x1, Pallas kernels: none -> 710 us  [body(): pl.pallas_call(_kernel, out_shape=[bf16((ROWS, D)), bf16((8, NC, HALF, W)...]
    all_gather x3 -> x0, waiting for transfers between devices: 528 us -> none  [the longest x1 301 us: body(): xg = lax.all_gather(xn, 'tp', axis=0, tiled=True)]
    dot_general x2 -> x0, matrix products: 309 us -> none  [the longest x1 158 us: body(): yp = jnp.dot(h, w2f, preferred_element_type=jnp.float32)]
    convert_element_type x2 -> x0, other arithmetic: 23.5 us -> none  [the longest x1 12 us: body(): return (xf + y).astype(jnp.bfloat16)]
  transfers between devices with their start and end apart: 4 -> 0, of which waited for: 4 -> 0; matrix products, arithmetic and copies ran while one was open for 11% -> 0% of each run, Pallas kernels for 0% -> 0%
where the time goes in v1:
time: 718 us
  Pallas kernels  710 us (99%)
  local copies, waits for them, and re-layouts  7.89 us (1%)
    pallas_call x1, Pallas kernels, body(): pl.pallas_call(_kernel, out_shape=[bf16((ROWS, D)), bf16((8, NC, HALF, W)...  710 us

profile of v1, /device:TPU:0, one launch (start us, length us, event | category | flops | bytes accessed | tf_op | source)
XLA Modules:
  0.0 717.5 jit_solution(17504054038919919166)
XLA Ops:
  0.0 709.6 %shard_map.46 = (bf16[1024,4096]{1,0:T(8,128)(2,1)}, bf16[8,8,2048,256]{3,2,1,0:T(8,128)(2,1)}, bf16[8,8,2048,256]{3,2,1,0:T(8,128)(2,1)}, bf16[1024,4096]{1,0:T...) custom-call(bf16[1024,4096]{1,0:T(8,128)(2,1)} %x.1, f32[1,4096]{1,0:T(1,128)} %bitcast.1, ...), custom_call_target="tpu_custom_call" | custom-call | flops 275000000512 | bytes 400000000 | tf_op jit(solution)/shard_map/pallas_call | solution.py:315
  709.6 7.9 %copy.6 = bf16[1024,4096]{1,0:T(8,128)(2,1)} copy(bf16[1024,4096]{1,0:T(8,128)(2,1)} %get-tuple-element.6) | data formatting | bytes 16777216

commit v2 on v1

--- a/solution.py
+++ b/solution.py
@@ -120,75 +120,146 @@
     xn_out(nx - 1).wait()
     xn_send(nx - 1).start()
 
-    def first(xn):
-        def load_tokens(src, row):
-            for k, at in enumerate((mine, other)):
-                pltpu.make_async_copy(
-                    src.at[:, pl.ds(at, HALF)], xn.at[pl.ds(row, ROWS), pl.ds(k * HALF, HALF)], loc.at[k]
-                ).start()
-            for k, at in enumerate((mine, other)):
-                pltpu.make_async_copy(
-                    src.at[:, pl.ds(at, HALF)], xn.at[pl.ds(row, ROWS), pl.ds(k * HALF, HALF)], loc.at[k]
-                ).wait()
-
-        load_tokens(xnh, 0)
-
-        def tiles(s, c, n, row, rows, new):
-            def load(q, k):
-                cc, sib = c + q // 2, SIB * (q % 2)
-                src = w1.at[:, cols(cc)] if (sib, k, s) == (0, 0, 0) else g1.at[sib + 2 * k + s, cc]
-                return pltpu.make_async_copy(src, wt.at[q, pl.ds(k * HALF, HALF)], loc.at[2 * q + k])
-
-            for q in range(2 * n):
+    def first(xn, pre):
+        def load_tokens(src, at, row, rows):
+            def part(k, column):
+                return pltpu.make_async_copy(
+                    src.at[pl.ds(at, rows), pl.ds(column, HALF)],
+                    xn.at[pl.ds(row, rows), pl.ds(k * HALF, HALF)],
+                    loc.at[k],
+                )
+
+            for k, column in enumerate((mine, other)):
+                part(k, column).start()
+            for k, column in enumerate((mine, other)):
+                part(k, column).wait()
+
+        def load(unit, slot, q, wait):
+            s, by_core, c, core = unit
+            cc, cr = c + by_core * q, (1 - by_core) * q + by_core * core
+
+            def start(src, k):
+                pltpu.make_async_copy(src, wt.at[slot, pl.ds(k * HALF, HALF)], loc.at[2 * slot + k]).start()
+
+            @pl.when((cr == 0) & (s == 0))
+            def _():
+                start(w1.at[:, cols(cc)], 0)
+
+            @pl.when((cr == 0) & (s == 1))
+            def _():
+                start(g1.at[Y, cc], 0)
+
+            @pl.when(cr == 0)
+            def _():
+                start(g1.at[Z + s, cc], 1)
+
+            @pl.when(cr == 1)
+            def _():
                 for k in range(2):
-                    if new and q % 2:
-                        arrived(0, SIB + 2 * k + s, c + q // 2)
-                    load(q, k).start()
-            nb = rows // BM
-
-            def product(i, _):
-                q, b = i // nb, lax.rem(i, nb)
-                for qq in range(2 * n):
-
-                    @pl.when(i == qq * nb)
-                    def _(qq=qq):
+
+                    @pl.when(wait)
+                    def _(k=k):
+                        arrived(0, SIB + 2 * k + s, cc)
+
+                    start(g1.at[SIB + 2 * k + s, cc], k)
+
+        def store_last(last):
+            row, column = last
+            at = pl.ds(pl.multiple_of(row, BM), BM), pl.ds(pl.multiple_of(column, W), W)
+            h[at] = jax.nn.gelu(pre[...], approximate=True).astype(jnp.bfloat16)
+
+        def run(n, unit, rows, ready, wait, last, ahead=lambda i: 0):
+            def load_unit(i):
+                ready(i)
+                for q in range(2):
+                    load(unit(i), 2 * lax.rem(i, 2) + q, q, wait(i))
+
+            def one(i, last):
+                pl.when((i == 0) | (i * 0 + ahead(i) < 0))(lambda: load_unit(i))
+                s, by_core, c, core = unit(i)
+                b0, nb = rows(i)
+
+                def product(m, last):
+                    q, b = m // nb, lax.rem(m, nb)
+                    slot = 2 * lax.rem(i, 2) + q
+
+                    @pl.when(b == 0)
+                    def _():
                         for k in range(2):
-                            load(qq, k).wait()
-
-                r = pl.ds(pl.multiple_of(row + b * BM, BM), BM)
-                pre = jnp.dot(xn[r, :], wt[q], preferred_element_type=jnp.float32)
-                at = (lax.rem(q, 2) * 2 + s) * HALF + (c + q // 2) * W
-                h[r, pl.ds(pl.multiple_of(at, W), W)] = jax.nn.gelu(pre, approximate=True).astype(jnp.bfloat16)
-                return 0
-
-            lax.fori_loop(0, 2 * n * nb, product, 0)
-
-        for g in range(3):
-            slot_a(0, g)
-            tiles(0, 2 * g + 1, 1, 0, ROWS, True)
-            slot_b(0, g)
-            tiles(0, 2 * g, 1, 0, ROWS, True)
-            if g < 2:
-                slot_c(0, g)
-                tiles(1, 2 * g, 2, 0, ROWS, True)
-        for i in range(nx):
+                            pltpu.make_async_copy(
+                                g1.at[Y, 0], wt.at[slot, pl.ds(k * HALF, HALF)], loc.at[2 * slot + k]
+                            ).wait()
+
+                    pl.when((i + 1 < n) & (m == ahead(i + 1)))(lambda: load_unit(i + 1))
+                    row = (b0 + b) * BM
+                    column = (((1 - by_core) * q + by_core * core) * 2 + s) * HALF + (c + by_core * q) * W
+                    store_last(last)
+                    r = pl.ds(pl.multiple_of(row, BM), BM)
+                    pre[...] = jnp.dot(xn[r, :], wt[slot], preferred_element_type=jnp.float32)
+                    return row, column
+
+                return lax.fori_loop(0, 2 * nb, product, last)
+
+            return lax.fori_loop(0, n, one, last)
+
+        load_tokens(xnh, 0, 0, ROWS)
+        zero = lax.rem(core, 1)
+        last = (zero, zero + W)
+        yes, no = (lambda i: i >= 0), (lambda i: i < 0)
+        nothing = lambda i: None
+
+        slot_a(0, 0)
+        last = run(1, lambda i: (0, 0, 1, 0), lambda i: (0, 2), nothing, yes, last)
+        slot_b(0, 0)
+        last = run(1, lambda i: (0, 0, 0, 0), lambda i: (0, 2), nothing, yes, last)
+        slot_c(0, 0)
+        last = run(2, lambda i: (1, 1, 0, i), lambda i: (0, 2), nothing, yes, last, lambda i: 2)
+        slot_a(0, 1)
+        last = run(1, lambda i: (0, 0, 3, 0), lambda i: (0, 2), nothing, yes, last)
+        for i in range(nx // 2):
             xn_send(i).wait_recv()
-        load_tokens(xph, ROWS)
-        for s in range(2):
-            tiles(s, 0, 2, ROWS, ROWS, False)
-        slot_c(0, 2)
-        for s in range(2):
-            tiles(s, 2, 2, ROWS, ROWS, False)
-        tiles(1, 4, 2, 0, 2 * ROWS, True)
-        slot_a(0, 3)
-        tiles(0, 4, 2, ROWS, ROWS, False)
-        tiles(0, 7, 1, 0, 2 * ROWS, True)
-        slot_b(0, 3)
-        tiles(0, 6, 1, 0, 2 * ROWS, True)
-        slot_c(0, 3)
-        tiles(1, 6, 2, 0, 2 * ROWS, True)
-
-    pl.run_scoped(first, pltpu.VMEM((2 * ROWS, D), jnp.bfloat16))
+        load_tokens(xph, 0, ROWS, ROWS // 2)
+        last = run(4, lambda i: (i // 2, 0, lax.rem(i, 2), 0), lambda i: (2, 1), nothing, no, last)
+        slot_b(0, 1)
+        last = run(1, lambda i: (0, 0, 2, 0), lambda i: (0, 3), nothing, yes, last)
+        last = run(1, lambda i: (0, 0, 3, 0), lambda i: (2, 1), nothing, no, last)
+        slot_c(0, 1)
+        last = run(2, lambda i: (1, 1, 2, i), lambda i: (0, 3), nothing, yes, last, lambda i: 3)
+        slot_a(0, 2)
+        last = run(1, lambda i: (0, 0, 5, 0), lambda i: (0, 3), nothing, yes, last)
+        slot_b(0, 2)
+        last = run(1, lambda i: (0, 0, 4, 0), lambda i: (0, 3), nothing, yes, last)
+        for i in range(nx // 2, nx):
+            xn_send(i).wait_recv()
+        load_tokens(xph, ROWS // 2, ROWS + ROWS // 2, ROWS // 2)
+
+        def unit(i):
+            late = i >= 10
+            s = jnp.where(late, jnp.where((i == 12) | (i == 13), 0, 1), lax.rem(i // 2, 2))
+            s = jnp.where((i == 8) | (i == 9), 0, s)
+            by_core = jnp.where(late & (s == 1), 1, 0)
+            c = jnp.where(i < 8, 2 * (i // 4) + lax.rem(i, 2), i - 4)
+            c = jnp.where(i >= 10, 4, c)
+            c = jnp.where(i == 12, 7, c)
+            c = jnp.where(i >= 13, 6, c)
+            return s, by_core, c, lax.rem(i, 2)
+
+        def rows(i):
+            return jnp.where(i >= 10, 0, 3), jnp.where(i >= 10, 4, 1)
+
+        def ready(i):
+            pl.when(i == 10)(lambda: slot_c(0, 2))
+            pl.when(i == 12)(lambda: slot_a(0, 3))
+            pl.when(i == 13)(lambda: slot_b(0, 3))
+            pl.when(i == 14)(lambda: slot_c(0, 3))
+
+        def ahead(i):
+            return jnp.where(i < 12, 0, jnp.where((i == 12) | (i == 15), 4, -1))
+
+        last = run(16, unit, rows, ready, lambda i: i >= 10, last, ahead)
+        store_last(last)
+
+    pl.run_scoped(first, pltpu.VMEM((2 * ROWS, D), jnp.bfloat16), pltpu.VMEM((BM, W), jnp.float32))
 
     def second(theirs, own, back, xb, yb):
         def where(j):

time: 718 us -> 690 us (0.961)
  Pallas kernels: 710 us -> 681 us
    pallas_call x1, Pallas kernels: 710 us -> 681 us  [body(): pl.pallas_call(_kernel, out_shape=[bf16((ROWS, D)), bf16((8, NC, HALF, W)...]
where the time goes in v2:
time: 690 us; the launch traced here: 689 us
  Pallas kernels  681 us (99%)
  local copies, waits for them, and re-layouts  7.89 us (1%)
    pallas_call x1, Pallas kernels, body(): pl.pallas_call(_kernel, out_shape=[bf16((ROWS, D)), bf16((8, NC, HALF, W)...  681 us

profile of v2, /device:TPU:0, one launch (start us, length us, event | category | flops | bytes accessed | tf_op | source)
XLA Modules:
  0.0 688.8 jit_solution(9447890115426346217)
XLA Ops:
  0.0 680.9 %shard_map.46 = (bf16[1024,4096]{1,0:T(8,128)(2,1)}, bf16[8,8,2048,256]{3,2,1,0:T(8,128)(2,1)}, bf16[8,8,2048,256]{3,2,1,0:T(8,128)(2,1)}, bf16[1024,4096]{1,0:T...) custom-call(bf16[1024,4096]{1,0:T(8,128)(2,1)} %x.1, f32[1,4096]{1,0:T(1,128)} %bitcast.1, ...), custom_call_target="tpu_custom_call" | custom-call | flops 275000000512 | bytes 400000000 | tf_op jit(solution)/shard_map/pallas_call | solution.py:386
  680.9 7.9 %copy.6 = bf16[1024,4096]{1,0:T(8,128)(2,1)} copy(bf16[1024,4096]{1,0:T(8,128)(2,1)} %get-tuple-element.6) | data formatting | bytes 16777216

commit v3 on v2

--- a/solution.py
+++ b/solution.py
@@ -17,10 +17,11 @@
 BM = 512
 XR = 256
 LAG = 3
+SLOTS = 2
 Y, Z, DIAG, SIB = 1, 2, 3, 4
 
 
-def _kernel(x, gamma, w1, w2, y, g1, g2, xnh, xph, rbuf, h, wt, send, recv, xsend, xrecv, psend, precv, loc):
+def _kernel(x, gamma, w1, w2, y, g1, g2, xnh, xph, rbuf, h, wt, send, recv, xsend, xrecv, psend, precv, ysend, yrecv, loc):
     f, t = lax.axis_index("fsdp"), lax.axis_index("tp")
     core, ix, iy = lax.rem(t, 2), lax.rem(t // 2, 2), t // 4
     to_core, to_x, to_y, to_z = (f, t + 1 - 2 * core), (f, t + 2 - 4 * ix), (f, t + 4 - 8 * iy), (1 - f, t)
@@ -49,25 +50,46 @@
         at = got[w].at[piece, c]
         pltpu.make_async_copy(at, at, recv.at[w, piece - 1, c]).wait()
 
+    def half_cols(u):
+        return pl.ds(u * (W // 2), W // 2)
+
+    def y_half(u):
+        return pltpu.make_async_remote_copy(
+            src_ref=w2.at[:, half_cols(u)], dst_ref=g2.at[Y, 0, :, half_cols(u)], send_sem=ysend.at[u],
+            recv_sem=yrecv.at[u], device_id=to_y, device_id_type=MESH,
+        )
+
+    def y_half_to_sib(u):
+        return pltpu.make_async_remote_copy(
+            src_ref=g2.at[Y, 0, :, half_cols(u)], dst_ref=g2.at[SIB + Y, 0, :, half_cols(u)], send_sem=ysend.at[2 + u],
+            recv_sem=yrecv.at[2 + u], device_id=to_core, device_id_type=MESH,
+        )
+
     def send_own(w, g):
         for k in range(2):
-            copy(w, 0, 0, Y, 2 * g + k, to_y).start()
+            if w == 1 and k == 0 and isinstance(g, int):
+                y_half(0).start()
+                y_half(1).start()
+            else:
+                copy(w, 0, 0, Y, 2 * g + k, to_y).start()
             copy(w, 1, 0, Z, 2 * g + 1 - k, to_z).start()
             copy(w, 2, 0, SIB, 2 * g + k, to_core).start()
 
     def to_sib(w, piece, c):
         copy(w, 2 + piece, piece, SIB + piece, c, to_core).start()
 
-    def slot_a(w, g):
-        arrived(w, Y, 2 * g)
+    def slot_a(w, g, halves=False):
+        if not halves:
+            arrived(w, Y, 2 * g)
         arrived(w, Z, 2 * g + 1)
         copy(w, 6, Z, DIAG, 2 * g + 1, to_y).start()
         copy(w, 6, Y, DIAG, 2 * g, to_z).start()
         if w == 0:
             send_own(*((0, g + 1) if g < 3 else (1, 0)))
         else:
-            pl.when(g < 3)(lambda: send_own(1, g + 1))
-        to_sib(w, Y, 2 * g)
+            pl.when(g < 3)(lambda: send_own(1, g + 1 + core * 0))
+        if not halves:
+            to_sib(w, Y, 2 * g)
         to_sib(w, Z, 2 * g + 1)
 
     def slot_b(w, g):
@@ -120,7 +142,7 @@
     xn_out(nx - 1).wait()
     xn_send(nx - 1).start()
 
-    def first(xn, pre):
+    def first(xn, pre, theirs):
         def load_tokens(src, at, row, rows):
             def part(k, column):
                 return pltpu.make_async_copy(
@@ -176,21 +198,28 @@
 
             def one(i, last):
                 pl.when((i == 0) | (i * 0 + ahead(i) < 0))(lambda: load_unit(i))
-                s, by_core, c, core = unit(i)
-                b0, nb = rows(i)
+                hook = lambda m: pl.when((i + 1 < n) & (m == ahead(i + 1)))(lambda: load_unit(i + 1))
+                return products(unit(i), 2 * lax.rem(i, 2), rows(i), last, hook)
+
+            return lax.fori_loop(0, n, one, last)
+
+        def products(unit, slot0, rows, last, hook=None):
+                s, by_core, c, core = unit
+                b0, nb = rows
 
                 def product(m, last):
                     q, b = m // nb, lax.rem(m, nb)
-                    slot = 2 * lax.rem(i, 2) + q
-
-                    @pl.when(b == 0)
+                    slot = slot0 + q
+
+                    @pl.when((b == 0) & (hook is not None))
                     def _():
                         for k in range(2):
                             pltpu.make_async_copy(
                                 g1.at[Y, 0], wt.at[slot, pl.ds(k * HALF, HALF)], loc.at[2 * slot + k]
                             ).wait()
 
-                    pl.when((i + 1 < n) & (m == ahead(i + 1)))(lambda: load_unit(i + 1))
+                    if hook is not None:
+                        hook(m)
                     row = (b0 + b) * BM
                     column = (((1 - by_core) * q + by_core * core) * 2 + s) * HALF + (c + by_core * q) * W
                     store_last(last)
@@ -199,8 +228,6 @@
                     return row, column
 
                 return lax.fori_loop(0, 2 * nb, product, last)
-
-            return lax.fori_loop(0, n, one, last)
 
         load_tokens(xnh, 0, 0, ROWS)
         zero = lax.rem(core, 1)
@@ -245,7 +272,7 @@
             return s, by_core, c, lax.rem(i, 2)
 
         def rows(i):
-            return jnp.where(i >= 10, 0, 3), jnp.where(i >= 10, 4, 1)
+            return jnp.where(i >= 10, jnp.where(i >= 14, 2, 0), 3), jnp.where(i >= 10, jnp.where(i >= 14, 2, 4), 1)
 
         def ready(i):
             pl.when(i == 10)(lambda: slot_c(0, 2))
@@ -254,47 +281,111 @@
             pl.when(i == 14)(lambda: slot_c(0, 3))
 
         def ahead(i):
-            return jnp.where(i < 12, 0, jnp.where((i == 12) | (i == 15), 4, -1))
+            return jnp.where(i < 12, 0, jnp.where(i == 12, 4, jnp.where(i == 15, 2, -1)))
 
         last = run(16, unit, rows, ready, lambda i: i >= 10, last, ahead)
-        store_last(last)
-
-    pl.run_scoped(first, pltpu.VMEM((2 * ROWS, D), jnp.bfloat16), pltpu.VMEM((BM, W), jnp.float32))
+
+        for u in range(2):
+            last = products((1, 1, 6, u), 2 * u, (0, 2), last)
+            store_last(last)
+            y_half(u).wait_recv()
+            y_half_to_sib(u).start()
+            pieces = (w2, g2.at[Y, 0], g2.at[SIB, 0], g2.at[SIB + Y, 0])
+            if u == 0:
+                arrived(1, SIB, 0)
+
+            def load_half(i, u=u):
+                src = w2.at[:, half_cols(u)] if i == 0 else pieces[i].at[:, half_cols(u)]
+                return pltpu.make_async_copy(
+                    src, wt.at[i // 2, pl.ds(i % 2 * HALF, HALF), half_cols(u)], loc.at[i]
+                )
+
+            for i in range(3):
+                load_half(i).start()
+            y_half_to_sib(u).wait_recv()
+            load_half(3).start()
+            for i in range(4):
+                load_half(i).wait()
+
+            def to_them(b, _, u=u):
+                r = pl.ds(pl.multiple_of(ROWS + b * BM, BM), BM)
+                theirs[0, pl.ds(pl.multiple_of(b * BM, BM), BM), half_cols(u)] = sum(
+                    jnp.dot(h[r, pl.ds(k * D, D)], wt[k, :, half_cols(u)], preferred_element_type=jnp.float32)
+                    for k in range(2)
+                )
+                return 0
+
+            lax.fori_loop(0, ROWS // BM, to_them, 0)
+            first_out(theirs, u).start()
+
+    def first_out(theirs, u):
+        return pltpu.make_async_remote_copy(
+            src_ref=theirs.at[0, :, half_cols(u)], dst_ref=rbuf.at[0, :, half_cols(u)], send_sem=psend.at[0, u],
+            recv_sem=precv.at[0, u], device_id=to_x, device_id_type=MESH,
+        )
+
+    def both(theirs):
+        pl.run_scoped(
+            functools.partial(first, theirs=theirs),
+            pltpu.VMEM((2 * ROWS, D), jnp.bfloat16),
+            pltpu.VMEM((BM, W), jnp.float32),
+        )
+        pl.run_scoped(
+            functools.partial(second, theirs),
+            pltpu.VMEM((LAG + 1, ROWS, W), jnp.float32),
+            pltpu.VMEM((ROWS, W), jnp.float32),
+            pltpu.VMEM((ROWS, W), jnp.bfloat16),
+            pltpu.VMEM((2, ROWS, W), jnp.bfloat16),
+        )
 
     def second(theirs, own, back, xb, yb):
         def where(j):
             r, c = lax.rem(j, 4) // 2, 2 * (j // 4) + lax.rem(j, 2)
             return r, c, pl.multiple_of(lax.rem(f + r, 2) * HALF + c * W, W)
 
-        def partial_out(j):
+        def half_rows(b):
+            return pl.ds(pl.multiple_of(b * BM, BM), BM)
+
+        def partial_out(j, b):
             return pltpu.make_async_remote_copy(
-                src_ref=theirs.at[lax.rem(j, LAG)], dst_ref=rbuf.at[j], send_sem=psend.at[j], recv_sem=precv.at[j],
-                device_id=to_x, device_id_type=MESH,
+                src_ref=theirs.at[lax.rem(j, SLOTS), half_rows(b)], dst_ref=rbuf.at[j, half_rows(b)],
+                send_sem=psend.at[j, b], recv_sem=precv.at[j, b], device_id=to_x, device_id_type=MESH,
             )
 
-        def y_out(j):
+        def y_out(j, b):
             _, _, at = where(j)
-            return pltpu.make_async_copy(yb.at[lax.rem(j, 2)], y.at[:, pl.ds(at, W)], loc.at[6 + lax.rem(j, 2)])
+            p = lax.rem(j, 2)
+            return pltpu.make_async_copy(
+                yb.at[p, half_rows(b)], y.at[half_rows(b), pl.ds(at, W)], loc.at[8 + 2 * p + b]
+            )
 
         def finish(j):
             _, _, at = where(j)
             a = pltpu.make_async_copy(x.at[:, pl.ds(at, W)], xb, loc.at[4])
-            b = pltpu.make_async_copy(rbuf.at[j], back, loc.at[5])
             a.start()
-            partial_out(j).wait_recv()
-            b.start()
-            pl.when(j >= 2)(lambda: y_out(j - 2).wait())
+            halves = [pltpu.make_async_copy(rbuf.at[j, half_rows(b)], back.at[half_rows(b)], loc.at[5 + b]) for b in range(2)]
+
+            @pl.when(j == 0)
+            def _():
+                for b in range(2):
+                    first_out(theirs, b).wait_recv()
+
+            for b in range(2):
+                pl.when(j > 0)(lambda b=b: partial_out(j, b).wait_recv())
+                halves[b].start()
+            pl.when(j >= 2)(lambda: [y_out(j - 2, b).wait() for b in range(2)] and None)
             a.wait()
-            b.wait()
-
-            def add(i, _):
-                r = pl.ds(pl.multiple_of(i * 64, 64), 64)
-                total = own[lax.rem(j, LAG + 1), r, :] + back[r, :]
-                yb[lax.rem(j, 2), r, :] = (xb[r, :].astype(jnp.float32) + total).astype(jnp.bfloat16)
-                return 0
-
-            lax.fori_loop(0, ROWS // 64, add, 0)
-            y_out(j).start()
+            for b in range(2):
+                halves[b].wait()
+
+                def add(i, _, b=b):
+                    r = pl.ds(pl.multiple_of(b * BM + i * 64, 64), 64)
+                    total = own[lax.rem(j, LAG + 1), r, :] + back[r, :]
+                    yb[lax.rem(j, 2), r, :] = (xb[r, :].astype(jnp.float32) + total).astype(jnp.bfloat16)
+                    return 0
+
+                lax.fori_loop(0, BM // 64, add, 0)
+                y_out(j, b).start()
 
         def product(row, b):
             r = pl.ds(pl.multiple_of(row + b * BM, BM), BM)
@@ -305,7 +396,8 @@
         def chunk(j, _):
             g, q = j // 4, lax.rem(j, 4)
             r, c, _ = where(j)
-            pl.when(q == 0)(lambda: slot_a(1, g))
+            pl.when(j == 0)(lambda: slot_a(1, 0 * g, True))
+            pl.when((q == 0) & (j > 0))(lambda: slot_a(1, g))
             pl.when(q == 1)(lambda: slot_b(1, g))
             pl.when(q == 2)(lambda: slot_c(1, g))
 
@@ -313,7 +405,7 @@
                 src = g2.at[SIB * sib + 2 * r + s, c]
                 return pltpu.make_async_copy(src, wt.at[sib, pl.ds(s * HALF, HALF)], loc.at[2 * sib + s])
 
-            @pl.when(r == 0)
+            @pl.when((r == 0) & (j > 0))
             def _():
                 pltpu.make_async_copy(w2.at[:, cols(c)], wt.at[0, pl.ds(0, HALF)], loc.at[0]).start()
 
@@ -321,21 +413,23 @@
             def _():
                 load(0, 0).start()
 
-            load(0, 1).start()
-            for s in range(2):
-                arrived(1, SIB + 2 * r + s, c)
-                load(1, s).start()
-            pl.when(j >= LAG)(lambda: partial_out(j - LAG).wait_send())
-            for sib in range(2):
+            @pl.when(j > 0)
+            def _():
+                load(0, 1).start()
                 for s in range(2):
-                    load(sib, s).wait()
-
-            def to_them(b, _):
-                theirs[lax.rem(j, LAG), pl.ds(pl.multiple_of(b * BM, BM), BM), :] = product(ROWS, b)
-                return 0
-
-            lax.fori_loop(0, ROWS // BM, to_them, 0)
-            partial_out(j).start()
+                    arrived(1, SIB + 2 * r + s, c)
+                    load(1, s).start()
+                pl.when(j >= SLOTS)(lambda: [partial_out(j - SLOTS, b).wait_send() for b in range(2)] and None)
+                for sib in range(2):
+                    for s in range(2):
+                        load(sib, s).wait()
+
+                def to_them(b, _):
+                    theirs[lax.rem(j, SLOTS), half_rows(b), :] = product(ROWS, b)
+                    partial_out(j, b).start()
+                    return 0
+
+                lax.fori_loop(0, ROWS // BM, to_them, 0)
 
             def to_us(b, _):
                 own[lax.rem(j, LAG + 1), pl.ds(pl.multiple_of(b * BM, BM), BM), :] = product(0, b)
@@ -349,29 +443,29 @@
 
         def drain(j, _):
             finish(j)
-            partial_out(j).wait_send()
             return 0
 
         lax.fori_loop(NJ - LAG, NJ, drain, 0)
         for j in range(NJ - 2, NJ):
-            y_out(j).wait()
-
-    pl.run_scoped(
-        second,
-        pltpu.VMEM((LAG, ROWS, W), jnp.float32),
-        pltpu.VMEM((LAG + 1, ROWS, W), jnp.float32),
-        pltpu.VMEM((ROWS, W), jnp.float32),
-        pltpu.VMEM((ROWS, W), jnp.bfloat16),
-        pltpu.VMEM((2, ROWS, W), jnp.bfloat16),
-    )
-
+            for b in range(2):
+                partial_out(j, b).wait_send()
+                y_out(j, b).wait()
+
+    pl.run_scoped(both, pltpu.VMEM((SLOTS, ROWS, W), jnp.float32))
+
+    for u in range(2):
+        y_half(u).wait_send()
+        y_half_to_sib(u).wait_send()
     for i in range(nx):
         xn_send(i).wait_send()
 
     def sent(c, _):
         for w in range(2):
             for kind in range(7):
-                copy(w, kind, Y, Y, c, to_y).wait_send()
+                if w == 1 and kind in (0, 3):
+                    pl.when(c > 0)(lambda kind=kind: copy(1, kind, Y, Y, c, to_y).wait_send())
+                else:
+                    copy(w, kind, Y, Y, c, to_y).wait_send()
         return 0
 
     lax.fori_loop(0, NC, sent, 0)
@@ -402,9 +496,11 @@
                 pltpu.SemaphoreType.DMA((2, 7, NC)),
                 pltpu.SemaphoreType.DMA((ROWS // XR,)),
                 pltpu.SemaphoreType.DMA((ROWS // XR,)),
-                pltpu.SemaphoreType.DMA((NJ,)),
-                pltpu.SemaphoreType.DMA((NJ,)),
-                pltpu.SemaphoreType.DMA((8,)),
+                pltpu.SemaphoreType.DMA((NJ, 2)),
+                pltpu.SemaphoreType.DMA((NJ, 2)),
+                pltpu.SemaphoreType.DMA((4,)),
+                pltpu.SemaphoreType.DMA((4,)),
+                pltpu.SemaphoreType.DMA((12,)),
             ],
             compiler_params=pltpu.CompilerParams(
                 collective_id=0, has_side_effects=True, vmem_limit_bytes=67_043_328

time: 690 us -> 683 us (0.990)
  Pallas kernels: 681 us -> 674 us
    pallas_call x1, Pallas kernels: 681 us -> 674 us  [body(): pl.pallas_call(_kernel, out_shape=[bf16((ROWS, D)), bf16((8, NC, HALF, W)...]
where the time goes in v3:
time: 683 us; the launch traced here: 682 us
  Pallas kernels  674 us (99%)
  local copies, waits for them, and re-layouts  7.89 us (1%)
    pallas_call x1, Pallas kernels, body(): pl.pallas_call(_kernel, out_shape=[bf16((ROWS, D)), bf16((8, NC, HALF, W)...  674 us

profile of v3, /device:TPU:0, one launch (start us, length us, event | category | flops | bytes accessed | tf_op | source)
XLA Modules:
  0.0 681.7 jit_solution(3994829723054659141)
XLA Ops:
  0.0 673.8 %shard_map.46 = (bf16[1024,4096]{1,0:T(8,128)(2,1)}, bf16[8,8,2048,256]{3,2,1,0:T(8,128)(2,1)}, bf16[8,8,2048,256]{3,2,1,0:T(8,128)(2,1)}, bf16[1024,4096]{1,0:T...) custom-call(bf16[1024,4096]{1,0:T(8,128)(2,1)} %x.1, f32[1,4096]{1,0:T(1,128)} %bitcast.1, ...), custom_call_target="tpu_custom_call" | custom-call | flops 275000000512 | bytes 400000000 | tf_op jit(solution)/shard_map/pallas_call | solution.py:480
  673.8 7.9 %copy.6 = bf16[1024,4096]{1,0:T(8,128)(2,1)} copy(bf16[1024,4096]{1,0:T(8,128)(2,1)} %get-tuple-element.6) | data formatting | bytes 16777216

commit v4 on v3

v4 whole, which is shorter than its diff:
```python
import functools

import jax
import jax.numpy as jnp
from jax import lax
from jax.experimental import pallas as pl
from jax.experimental.pallas import tpu as pltpu
from jax.sharding import PartitionSpec as P

EPS = 1e-6
MESH = pl.DeviceIdType.MESH

ROWS, D, HALF = 1024, 4096, 2048
W = 256
NC = HALF // W
NJ = 2 * NC
BM = 512
XR = 256
LAG = 3
SLOTS = 2
Y, Z, DIAG, SIB = 1, 2, 3, 4


def _kernel(x, gamma, w1, w2, y, o, g1, g2, xnh, xph, rbuf, h, wt, send, recv, xsend, xrecv, psend, precv, dsend, drecv, loc):
    f, t = lax.axis_index("fsdp"), lax.axis_index("tp")
    core, ix, iy = lax.rem(t, 2), lax.rem(t // 2, 2), t // 4
    to_core, to_x, to_y, to_z = (f, t + 1 - 2 * core), (f, t + 2 - 4 * ix), (f, t + 4 - 8 * iy), (1 - f, t)
    shard, got = (w1, w2), (g1, g2)
    mine, other = pl.multiple_of(f * HALF, HALF), pl.multiple_of((1 - f) * HALF, HALF)

    barrier = pltpu.get_barrier_semaphore()
    for d in (to_core, to_x, to_y, to_z):
        pl.semaphore_signal(barrier, inc=1, device_id=d, device_id_type=MESH)
    pl.semaphore_wait(barrier, 4)

    def cols(c):
        return pl.ds(pl.multiple_of(c * W, W), W)

    def copy(w, kind, src, dst_piece, c, device):
        return pltpu.make_async_remote_copy(
            src_ref=shard[w].at[:, cols(c)] if src == 0 else got[w].at[src, c],
            dst_ref=got[w].at[dst_piece, c],
            send_sem=send.at[w, kind, c],
            recv_sem=recv.at[w, dst_piece - 1, c],
            device_id=device,
            device_id_type=MESH,
        )

    def arrived(w, piece, c):
        at = got[w].at[piece, c]
        pltpu.make_async_copy(at, at, recv.at[w, piece - 1, c]).wait()

    def diag_half(k):
        piece, device = ((Z, to_y), (Y, to_z))[k]
        rows = pl.ds(k * HALF // 2, HALF // 2)
        return pltpu.make_async_remote_copy(
            src_ref=g1.at[piece, NC - 1, rows], dst_ref=g1.at[DIAG, NC - 1, rows], send_sem=dsend.at[k],
            recv_sem=drecv.at[k], device_id=device, device_id_type=MESH,
        )

    def own_to_y(w, c):
        copy(w, 0, 0, Y, c, to_y).start()
        copy(w, 2, 0, SIB, c, to_core).start()

    def own_to_z(w, c):
        copy(w, 1, 0, Z, c, to_z).start()

    def to_sib(w, piece, c):
        copy(w, 2 + piece, piece, SIB + piece, c, to_core).start()

    def slot_a(g):
        arrived(0, Y, 2 * g)
        arrived(0, Z, 2 * g + 1)
        copy(0, 6, Y, DIAG, 2 * g, to_z).start()
        if g < 3:
            copy(0, 6, Z, DIAG, 2 * g + 1, to_y).start()
            for k in (2, 3):
                own_to_y(0, 2 * g + k)
                own_to_z(0, 2 * g + 5 - k)
        else:
            diag_half(0).start()
            for c in range(3):
                own_to_y(1, c)
        to_sib(0, Y, 2 * g)
        to_sib(0, Z, 2 * g + 1)

    def slot_b(g):
        arrived(0, Y, 2 * g + 1)
        arrived(0, Z, 2 * g)
        if g == 3:
            diag_half(1).start()
            own_to_z(1, 1)
            own_to_z(1, 0)
        to_sib(0, Y, 2 * g + 1)
        to_sib(0, Z, 2 * g)

    def slot_c(g):
        for c in (2 * g, 2 * g + 1):
            arrived(0, DIAG, c)
            to_sib(0, DIAG, c)

    for c in range(2):
        own_to_y(0, c)
        own_to_z(0, 1 - c)

    def x_in(i):
        return pltpu.make_async_copy(x.at[pl.ds(i * XR, XR)], h.at[pl.ds(i * XR, XR), pl.ds(0, D)], loc.at[i])

    def xn_out(i):
        return pltpu.make_async_copy(h.at[pl.ds(i * XR, XR), pl.ds(0, D)], xnh.at[pl.ds(i * XR, XR)], loc.at[4 + i])

    def xn_send(i):
        rows = pl.ds(i * XR, XR)
        return pltpu.make_async_remote_copy(
            src_ref=xnh.at[rows], dst_ref=xph.at[rows], send_sem=xsend.at[i], recv_sem=xrecv.at[i],
            device_id=to_x, device_id_type=MESH,
        )

    nx = ROWS // XR
    for i in range(nx):
        x_in(i).start()
    for i in range(nx):
        x_in(i).wait()

        def norm(b, _, i=i):
            rows = pl.ds(pl.multiple_of(i * XR + b * 16, 16), 16)
            xf = h[rows, pl.ds(0, D)].astype(jnp.float32)
            mu = jnp.mean(xf, axis=-1, keepdims=True)
            xc = xf - mu
            var = jnp.mean(jnp.square(xc), axis=-1, keepdims=True)
            h[rows, pl.ds(0, D)] = (xc * lax.rsqrt(var + EPS) * gamma[...]).astype(jnp.bfloat16)
            return _

        lax.fori_loop(0, XR // 16, norm, 0)
        xn_out(i).start()
        if i > 0:
            xn_out(i - 1).wait()
            xn_send(i - 1).start()
    xn_out(nx - 1).wait()
    xn_send(nx - 1).start()

    def first(xn, pre, theirs):
        def load_tokens(src, at, row, rows):
            def part(k, column):
                return pltpu.make_async_copy(
                    src.at[pl.ds(at, rows), pl.ds(column, HALF)],
                    xn.at[pl.ds(row, rows), pl.ds(k * HALF, HALF)],
                    loc.at[k],
                )

            for k, column in enumerate((mine, other)):
                part(k, column).start()
            for k, column in enumerate((mine, other)):
                part(k, column).wait()

        def load(unit, slot, q, wait):
            s, by_core, c, core = unit
            cc, cr = c + by_core * q, (1 - by_core) * q + by_core * core

            def start(src, k):
                pltpu.make_async_copy(src, wt.at[slot, pl.ds(k * HALF, HALF)], loc.at[2 * slot + k]).start()

            @pl.when((cr == 0) & (s == 0))
            def _():
                start(w1.at[:, cols(cc)], 0)

            @pl.when((cr == 0) & (s == 1))
            def _():
                start(g1.at[Y, cc], 0)

            @pl.when(cr == 0)
            def _():
                start(g1.at[Z + s, cc], 1)

            @pl.when(cr == 1)
            def _():
                for k in range(2):

                    @pl.when(wait)
                    def _(k=k):
                        arrived(0, SIB + 2 * k + s, cc)

                    start(g1.at[SIB + 2 * k + s, cc], k)

        def store_last(last):
            row, column = last
            at = pl.ds(pl.multiple_of(row, BM), BM), pl.ds(pl.multiple_of(column, W), W)
            h[at] = jax.nn.gelu(pre[...], approximate=True).astype(jnp.bfloat16)

        def run(n, unit, rows, ready, wait, last, ahead=lambda i: 0):
            def load_unit(i):
                ready(i)
                for q in range(2):
                    load(unit(i), 2 * lax.rem(i, 2) + q, q, wait(i))

            def one(i, last):
                pl.when((i == 0) | (i * 0 + ahead(i) < 0))(lambda: load_unit(i))
                hook = lambda m: pl.when((i + 1 < n) & (m == ahead(i + 1)))(lambda: load_unit(i + 1))
                return products(unit(i), 2 * lax.rem(i, 2), rows(i), last, hook)

            return lax.fori_loop(0, n, one, last)

        def products(unit, slot0, rows, last, hook=None):
                s, by_core, c, core = unit
                b0, nb = rows

                def product(m, last):
                    q, b = m // nb, lax.rem(m, nb)
                    slot = slot0 + q

                    @pl.when((b == 0) & (hook is not None))
                    def _():
                        for k in range(2):
                            pltpu.make_async_copy(
                                g1.at[Y, 0], wt.at[slot, pl.ds(k * HALF, HALF)], loc.at[2 * slot + k]
                            ).wait()

                    if hook is not None:
                        hook(m)
                    row = (b0 + b) * BM
                    column = (((1 - by_core) * q + by_core * core) * 2 + s) * HALF + (c + by_core * q) * W
                    store_last(last)
                    r = pl.ds(pl.multiple_of(row, BM), BM)
                    pre[...] = jnp.dot(xn[r, :], wt[slot], preferred_element_type=jnp.float32)
                    return row, column

                return lax.fori_loop(0, 2 * nb, product, last)

        load_tokens(xnh, 0, 0, ROWS)
        zero = lax.rem(core, 1)
        last = (zero, zero + W)
        own_rows, three, early = (0, 2), (0, 3), (2, 1)
        yes, no = (lambda i: i >= 0), (lambda i: i < 0)
        nothing = lambda i: None

        slot_a(0)
        last = run(1, lambda i: (0, 0, 1, 0), lambda i: own_rows, nothing, yes, last)
        slot_b(0)
        last = run(1, lambda i: (0, 0, 0, 0), lambda i: own_rows, nothing, yes, last)
        slot_c(0)
        last = run(2, lambda i: (1, 1, 0, i), lambda i: own_rows, nothing, yes, last, lambda i: 2)
        slot_a(1)
        last = run(1, lambda i: (0, 0, 3, 0), lambda i: own_rows, nothing, yes, last)
        for i in range(nx // 2):
            xn_send(i).wait_recv()
        load_tokens(xph, 0, ROWS, ROWS // 2)
        last = run(4, lambda i: (i // 2, 0, lax.rem(i, 2), 0), lambda i: early, nothing, no, last)
        slot_b(1)
        last = run(1, lambda i: (0, 0, 2, 0), lambda i: three, nothing, yes, last)
        last = run(1, lambda i: (0, 0, 3, 0), lambda i: early, nothing, no, last)
        slot_c(1)
        last = run(2, lambda i: (1, 1, 2, i), lambda i: three, nothing, yes, last, lambda i: 3)
        slot_a(2)
        last = run(1, lambda i: (0, 0, 5, 0), lambda i: three, nothing, yes, last)
        slot_b(2)
        last = run(1, lambda i: (0, 0, 4, 0), lambda i: three, nothing, yes, last)
        for i in range(nx // 2, nx):
            xn_send(i).wait_recv()
        load_tokens(xph, ROWS // 2, ROWS + ROWS // 2, ROWS // 2)

        def unit(i):
            late = i >= 10
            s = jnp.where(late, jnp.where((i == 12) | (i == 13), 0, 1), lax.rem(i // 2, 2))
            s = jnp.where((i == 8) | (i == 9), 0, s)
            by_core = jnp.where(late & (s == 1), 1, 0)
            c = jnp.where(i < 8, 2 * (i // 4) + lax.rem(i, 2), i - 4)
            c = jnp.where(i >= 10, 4, c)
            c = jnp.where(i == 12, 7, c)
            c = jnp.where(i >= 13, 6, c)
            return s, by_core, c, lax.rem(i, 2)

        def rows(i):
            return jnp.where(i >= 10, 0, 3), jnp.where(i >= 10, 4, 1)

        def ready(i):
            pl.when(i == 10)(lambda: slot_c(2))
            pl.when(i == 12)(lambda: slot_a(3))
            pl.when(i == 13)(lambda: slot_b(3))

        def ahead(i):
            return jnp.where(i < 12, 0, jnp.where(i == 12, 4, -1))

        last = run(14, unit, rows, ready, lambda i: i >= 10, last, ahead)

        arrived(0, DIAG, NC - 2)
        to_sib(0, DIAG, NC - 2)
        u = (1, 0, NC - 2, 0)
        load(u, 0, 0, True)
        last = products(u, 0, (0, 4), last, lambda m: pl.when(m == 1)(lambda: load(u, 1, 1, True)))

        for k in range(2):
            diag_half(k).wait_recv()
        to_sib(0, DIAG, NC - 1)
        v = (1, 0, NC - 1, 0)
        load(v, 2, 0, True)
        arrived(1, Y, 0)
        to_sib(1, Y, 0)
        arrived(1, SIB, 0)
        pieces = (w2.at[:, cols(0)], g2.at[Y, 0], g2.at[SIB, 0], g2.at[SIB + Y, 0])

        def load_piece(i):
            return pltpu.make_async_copy(pieces[i], wt.at[i // 2, pl.ds(i % 2 * HALF, HALF)], loc.at[i])

        for i in range(3):
            load_piece(i).start()

        def last_piece():
            arrived(1, SIB + Y, 0)
            load_piece(3).start()

        def hook(m):
            pl.when(m == 1)(lambda: load(v, 3, 1, True))
            pl.when(m == 3)(last_piece)

        last = products(v, 2, (2, 2), last, hook)
        store_last(last)
        for i in range(4):
            load_piece(i).wait()
        partials(theirs, 0)
        last = products(v, 2, own_rows, last)
        store_last(last)

    def half_rows(b):
        return pl.ds(pl.multiple_of(b * BM, BM), BM)

    def partial_out(theirs, j, b):
        return pltpu.make_async_remote_copy(
            src_ref=theirs.at[lax.rem(j, SLOTS), half_rows(b)], dst_ref=rbuf.at[j, half_rows(b)],
            send_sem=psend.at[j, b], recv_sem=precv.at[j, b], device_id=to_x, device_id_type=MESH,
        )

    def second_product(row, b):
        r = pl.ds(pl.multiple_of(row + b * BM, BM), BM)
        return sum(jnp.dot(h[r, pl.ds(k * D, D)], wt[k], preferred_element_type=jnp.float32) for k in range(2))

    def partials(theirs, j):
        def to_them(b, _):
            theirs[lax.rem(j, SLOTS), half_rows(b), :] = second_product(ROWS, b)
            partial_out(theirs, j, b).start()
            return _

        lax.fori_loop(0, ROWS // BM, to_them, 0)

    def both(theirs):
        pl.run_scoped(
            functools.partial(first, theirs=theirs),
            pltpu.VMEM((2 * ROWS, D), jnp.bfloat16),
            pltpu.VMEM((BM, W), jnp.float32),
        )
        pl.run_scoped(
            functools.partial(second, theirs),
            pltpu.VMEM((LAG + 1, ROWS, W), jnp.float32),
            pltpu.VMEM((ROWS, W), jnp.float32),
            pltpu.VMEM((ROWS, W), jnp.bfloat16),
            pltpu.VMEM((2, ROWS, W), jnp.bfloat16),
        )

    def second(theirs, own, back, xb, yb):
        def where(j):
            g, q = (j + 3) // 4 - 1, lax.rem(j + 3, 4)
            r = jnp.where(j >= 14, 1, q // 2)
            c = jnp.where(j >= 14, j - 8, 2 * g + jnp.where(q < 2, q + 1, q - 2))
            r, c = jnp.where(j == 0, 0, r), jnp.where(j == 0, 0, c)
            return r, c, pl.multiple_of(lax.rem(f + r, 2) * HALF + c * W, W)

        def y_out(j, b):
            _, _, at = where(j)
            p = lax.rem(j, 2)
            return pltpu.make_async_copy(
                yb.at[p, half_rows(b)], y.at[half_rows(b), pl.ds(at, W)], loc.at[8 + 2 * p + b]
            )

        def finish(j):
            _, _, at = where(j)
            a = pltpu.make_async_copy(x.at[:, pl.ds(at, W)], xb, loc.at[4])
            a.start()
            halves = [pltpu.make_async_copy(rbuf.at[j, half_rows(b)], back.at[half_rows(b)], loc.at[5 + b]) for b in range(2)]

            for b in range(2):
                partial_out(theirs, j, b).wait_recv()
                halves[b].start()
            pl.when(j >= 2)(lambda: [y_out(j - 2, b).wait() for b in range(2)] and None)
            a.wait()
            for b in range(2):
                halves[b].wait()

                def add(i, _, b=b):
                    r = pl.ds(pl.multiple_of(b * BM + i * 64, 64), 64)
                    total = own[lax.rem(j, LAG + 1), r, :] + back[r, :]
                    yb[lax.rem(j, 2), r, :] = (xb[r, :].astype(jnp.float32) + total).astype(jnp.bfloat16)
                    return _

                lax.fori_loop(0, BM // 64, add, 0)
                y_out(j, b).start()

        def chunk(j, carry):
            g, q = (j + 3) // 4 - 1, lax.rem(j + 3, 4)
            r, c, _ = where(j)

            even = 2 * g
            odd = even + 1

            @pl.when((j > 0) & (q == 0))
            def _():
                arrived(1, Y, odd)
                arrived(1, Z, odd)
                copy(1, 6, Z, DIAG, odd, to_y).start()
                copy(1, 6, Y, DIAG, even, to_z).start()

                @pl.when(g < 3)
                def _():
                    own_to_y(1, odd + 2)
                    own_to_z(1, odd + 2)
                    own_to_z(1, even + 2)

                pl.when(g < 2)(lambda: own_to_y(1, odd + 3))
                to_sib(1, Y, odd)
                to_sib(1, Z, odd)

            @pl.when((j > 0) & (q == 1))
            def _():
                @pl.when(g < 3)
                def _():
                    arrived(1, Y, even + 2)
                    to_sib(1, Y, even + 2)

                arrived(1, Z, even)
                to_sib(1, Z, even)

            @pl.when((j > 0) & (((q == 2) & (g < 3)) | (j == 14)))
            def _():
                for k in range(2):
                    arrived(1, DIAG, even + k)
                    to_sib(1, DIAG, even + k)

            def load(sib, s):
                src = g2.at[SIB * sib + 2 * r + s, c]
                return pltpu.make_async_copy(src, wt.at[sib, pl.ds(s * HALF, HALF)], loc.at[2 * sib + s])

            @pl.when((r == 0) & (j > 0))
            def _():
                pltpu.make_async_copy(w2.at[:, cols(c)], wt.at[0, pl.ds(0, HALF)], loc.at[0]).start()

            @pl.when(r == 1)
            def _():
                load(0, 0).start()

            @pl.when(j > 0)
            def _():
                load(0, 1).start()
                for s in range(2):
                    arrived(1, SIB + 2 * r + s, c)
                    load(1, s).start()
                pl.when(j >= SLOTS)(lambda: [partial_out(theirs, j - SLOTS, b).wait_send() for b in range(2)] and None)
                for sib in range(2):
                    for s in range(2):
                        load(sib, s).wait()

                partials(theirs, j)

            def to_us(b, _):
                own[lax.rem(j, LAG + 1), pl.ds(pl.multiple_of(b * BM, BM), BM), :] = second_product(0, b)
                return _

            lax.fori_loop(0, ROWS // BM, to_us, 0)
            pl.when(j >= LAG)(lambda: finish(j - LAG))
            return carry

        lax.fori_loop(0, NJ, chunk, 0)

        def drain(j, _):
            finish(j)
            return _

        last = NJ - 1
        keep = pltpu.make_async_copy(own.at[last % (LAG + 1)], o, loc.at[0])
        keep.start()
        lax.fori_loop(NJ - LAG, last, drain, 0)
        keep.wait()
        for j in (last, last - 1):
            for b in range(2):
                partial_out(theirs, j, b).wait_send()
                y_out(j - 1, b).wait()
        for b in range(2):
            partial_out(theirs, last, b).wait_recv()

    pl.run_scoped(both, pltpu.VMEM((SLOTS, ROWS, W), jnp.float32))

    for u in range(2):
        diag_half(u).wait_send()
    for i in range(nx):
        xn_send(i).wait_send()

    def sent(c, _):
        for w in range(2):
            for kind in range(7):
                if w == 0 and kind == 6:
                    pl.when(c < NC - 1)(lambda: copy(0, 6, Y, Y, c, to_y).wait_send())
                else:
                    copy(w, kind, Y, Y, c, to_y).wait_send()
        return _

    lax.fori_loop(0, NC, sent, 0)


def _finish(at, x, o, r, y, out, rows, xv, ov, rv, small, came, went):
    n = came.shape[0]
    block = ROWS // n
    columns = pl.ds(pl.multiple_of(at[0], W), W)

    sums = [
        pltpu.make_async_copy(src, dst, small.at[k])
        for k, (src, dst) in enumerate(zip((x.at[:, columns], o, r.at[NJ - 1]), (xv, ov, rv)))
    ]

    def move(i, out_of):
        here, hbm = rows.at[pl.ds(i * block, block)], pl.ds(i * block, block)
        if out_of:
            return pltpu.make_async_copy(here, out.at[hbm], went.at[i])
        return pltpu.make_async_copy(y.at[hbm], here, came.at[i])

    for part in sums:
        part.start()
    for i in range(n):
        move(i, False).start()
    for part in sums:
        part.wait()
    for i in range(n):
        move(i, False).wait()
        b = pl.ds(i * block, block)
        rows[b, columns] = (xv[b, :].astype(jnp.float32) + (ov[b, :] + rv[b, :])).astype(jnp.bfloat16)
        move(i, True).start()
    for i in range(n):
        move(i, True).wait()


def solution(mesh):
    hbm = pl.BlockSpec(memory_space=pltpu.HBM)
    vmem = pl.BlockSpec(memory_space=pltpu.VMEM)

    def body(x, gamma, w1, w2):
        bf16 = functools.partial(jax.ShapeDtypeStruct, dtype=jnp.bfloat16)
        out = pl.pallas_call(
            _kernel,
            out_shape=[
                bf16((ROWS, D)),
                jax.ShapeDtypeStruct((ROWS, W), jnp.float32),
                bf16((8, NC, HALF, W)),
                bf16((8, NC, HALF, W)),
                bf16((ROWS, D)),
                bf16((ROWS, D)),
                jax.ShapeDtypeStruct((NJ, ROWS, W), jnp.float32),
            ],
            in_specs=[hbm, vmem, hbm, hbm],
            out_specs=[hbm] * 7,
            scratch_shapes=[
                pltpu.VMEM((2 * ROWS, 4 * HALF), jnp.bfloat16),
                pltpu.VMEM((4, D, W), jnp.bfloat16),
                pltpu.SemaphoreType.DMA((2, 7, NC)),
                pltpu.SemaphoreType.DMA((2, 7, NC)),
                pltpu.SemaphoreType.DMA((ROWS // XR,)),
                pltpu.SemaphoreType.DMA((ROWS // XR,)),
                pltpu.SemaphoreType.DMA((NJ, 2)),
                pltpu.SemaphoreType.DMA((NJ, 2)),
                pltpu.SemaphoreType.DMA((2,)),
                pltpu.SemaphoreType.DMA((2,)),
                pltpu.SemaphoreType.DMA((12,)),
            ],
            compiler_params=pltpu.CompilerParams(
                collective_id=0, has_side_effects=True, vmem_limit_bytes=67_043_328
            ),
            cost_estimate=pl.CostEstimate(flops=275_000_000_000, bytes_accessed=400_000_000, transcendentals=16_777_216),
        )(x, gamma.reshape(1, D), w1, w2)
        at = lax.rem(lax.axis_index("fsdp") + 1, 2) * HALF + HALF - W
        blocks = 8
        return pl.pallas_call(
            _finish,
            out_shape=bf16((ROWS, D)),
            in_specs=[pl.BlockSpec(memory_space=pltpu.SMEM)] + [hbm] * 4,
            out_specs=hbm,
            scratch_shapes=[
                pltpu.VMEM((ROWS, D), jnp.bfloat16),
                pltpu.VMEM((ROWS, W), jnp.bfloat16),
                pltpu.VMEM((ROWS, W), jnp.float32),
                pltpu.VMEM((ROWS, W), jnp.float32),
                pltpu.SemaphoreType.DMA((3,)),
                pltpu.SemaphoreType.DMA((blocks,)),
                pltpu.SemaphoreType.DMA((blocks,)),
            ],
        )(at.reshape(1), x, out[1], out[-1], out[0])

    return jax.shard_map(
        body,
        mesh=mesh,
        in_specs=(P(("fsdp", "tp"), None), P(None), P("fsdp", "tp"), P("tp", "fsdp")),
        out_specs=P(("fsdp", "tp"), None),
        check_vma=False,
    )
```

time: 683 us -> 677 us (level)
  local copies, waits for them, and re-layouts: 7.89 us -> 0 us
    unnamed x1 -> x0, local copies, waits for them, and re-layouts: 7.89 us -> none
    pallas_call x1 -> x2, Pallas kernels: 674 us -> 676 us  [the longest x1 669 us: body(): pl.pallas_call(_kernel, out_shape=[bf16((ROWS, D)), jax.ShapeDtypeStruct(...]
where the time goes in v4:
time: 677 us; the launch traced here: 676 us
  Pallas kernels  676 us (100%)
    pallas_call x1, Pallas kernels, body(): pl.pallas_call(_kernel, out_shape=[bf16((ROWS, D)), jax.ShapeDtypeStruct(...  669 us

profile of v4, /device:TPU:0, one launch (start us, length us, event | category | flops | bytes accessed | tf_op | source)
XLA Modules:
  0.0 676.2 jit_solution(12916034626602753728)
XLA Ops:
  0.0 668.7 %shard_map.46 = (bf16[1024,4096]{1,0:T(8,128)(2,1)}, f32[1024,256]{1,0:T(8,128)}, bf16[8,8,2048,256]{3,2,1,0:T(8,128)(2,1)}, bf16[8,8,2048,256]{3,2,1,0:T(8,128)...) custom-call(bf16[1024,4096]{1,0:T(8,128)(2,1)} %x.3, f32[1,4096]{1,0:T(1,128)} %bitcast.2, ...), custom_call_target="tpu_custom_call" | custom-call | flops 275000000512 | bytes 400000000 | tf_op jit(solution)/shard_map/pallas_call | solution.py:543
  668.7 7.3 %shard_map.47 = bf16[1024,4096]{1,0:T(8,128)(2,1)} custom-call(s32[1]{0:T(128)} %bitcast.at, bf16[1024,4096]{1,0:T(8,128)(2,1)} %x.3, f32[1024,256]{1,0:T(8,128)} %get-tuple-element.8.o, f32[16,1024,256]{2,1,0:T(8,128)} %get-tuple-element.9.r, bf16[1024,4096]{1,0:T(8,128)(2,1)} %get-tuple-element.10.y), custom_call_target="tpu_custom_call" | custom-call | tf_op jit(solution)/shard_map/pallas_call | solution.py:576

commit v5 on v4

--- a/solution.py
+++ b/solution.py
@@ -18,6 +18,7 @@
 XR = 256
 LAG = 3
 SLOTS = 2
+LINK, SIBLING = range(2)
 Y, Z, DIAG, SIB = 1, 2, 3, 4
 
 
@@ -50,13 +51,20 @@
         at = got[w].at[piece, c]
         pltpu.make_async_copy(at, at, recv.at[w, piece - 1, c]).wait()
 
-    def diag_half(k):
+    def diag_half(k, sib):
         piece, device = ((Z, to_y), (Y, to_z))[k]
+        if sib:
+            piece, device = DIAG, to_core
         rows = pl.ds(k * HALF // 2, HALF // 2)
+        i = 2 * sib + k
         return pltpu.make_async_remote_copy(
-            src_ref=g1.at[piece, NC - 1, rows], dst_ref=g1.at[DIAG, NC - 1, rows], send_sem=dsend.at[k],
-            recv_sem=drecv.at[k], device_id=device, device_id_type=MESH,
+            src_ref=g1.at[piece, NC - 1, rows], dst_ref=g1.at[SIB * sib + DIAG, NC - 1, rows], send_sem=dsend.at[i],
+            recv_sem=drecv.at[i], device_id=device, device_id_type=MESH,
         )
+
+    def pass_half(k):
+        diag_half(k, LINK).wait_recv()
+        diag_half(k, SIBLING).start()
 
     def own_to_y(w, c):
         copy(w, 0, 0, Y, c, to_y).start()
@@ -78,7 +86,7 @@
                 own_to_y(0, 2 * g + k)
                 own_to_z(0, 2 * g + 5 - k)
         else:
-            diag_half(0).start()
+            diag_half(0, LINK).start()
             for c in range(3):
                 own_to_y(1, c)
         to_sib(0, Y, 2 * g)
@@ -88,7 +96,7 @@
         arrived(0, Y, 2 * g + 1)
         arrived(0, Z, 2 * g)
         if g == 3:
-            diag_half(1).start()
+            diag_half(1, LINK).start()
             own_to_z(1, 1)
             own_to_z(1, 0)
         to_sib(0, Y, 2 * g + 1)
@@ -227,7 +235,7 @@
                 return lax.fori_loop(0, 2 * nb, product, last)
 
         load_tokens(xnh, 0, 0, ROWS)
-        zero = lax.rem(core, 1)
+        zero = core - core
         last = (zero, zero + W)
         own_rows, three, early = (0, 2), (0, 3), (2, 1)
         yes, no = (lambda i: i >= 0), (lambda i: i < 0)
@@ -284,13 +292,12 @@
 
         arrived(0, DIAG, NC - 2)
         to_sib(0, DIAG, NC - 2)
+        pass_half(0)
         u = (1, 0, NC - 2, 0)
         load(u, 0, 0, True)
         last = products(u, 0, (0, 4), last, lambda m: pl.when(m == 1)(lambda: load(u, 1, 1, True)))
 
-        for k in range(2):
-            diag_half(k).wait_recv()
-        to_sib(0, DIAG, NC - 1)
+        pass_half(1)
         v = (1, 0, NC - 1, 0)
         load(v, 2, 0, True)
         arrived(1, Y, 0)
@@ -308,8 +315,14 @@
             arrived(1, SIB + Y, 0)
             load_piece(3).start()
 
+        def other_tile():
+            arrived(0, SIB + Y, NC - 1)
+            for k in range(2):
+                diag_half(k, SIBLING).wait_recv()
+            load(v, 3, 1, core < 0)
+
         def hook(m):
-            pl.when(m == 1)(lambda: load(v, 3, 1, True))
+            pl.when(m == 1)(other_tile)
             pl.when(m == 3)(last_piece)
 
         last = products(v, 2, (2, 2), last, hook)
@@ -340,6 +353,24 @@
             return _
 
         lax.fori_loop(0, ROWS // BM, to_them, 0)
+
+    def settle():
+        for u in range(2):
+            diag_half(u, LINK).wait_send()
+            diag_half(u, SIBLING).wait_send()
+        for i in range(nx):
+            xn_send(i).wait_send()
+
+        def sent(c, _):
+            for w in range(2):
+                for kind in range(7):
+                    if w == 0 and kind > 4:
+                        pl.when(c < NC - 1)(lambda kind=kind: copy(0, kind, Y, Y, c, to_y).wait_send())
+                    else:
+                        copy(w, kind, Y, Y, c, to_y).wait_send()
+            return _
+
+        lax.fori_loop(0, NC, sent, 0)
 
     def both(theirs):
         pl.run_scoped(
@@ -403,6 +434,7 @@
             @pl.when((j > 0) & (q == 0))
             def _():
                 arrived(1, Y, odd)
+                to_sib(1, Y, odd)
                 arrived(1, Z, odd)
                 copy(1, 6, Z, DIAG, odd, to_y).start()
                 copy(1, 6, Y, DIAG, even, to_z).start()
@@ -414,7 +446,6 @@
                     own_to_z(1, even + 2)
 
                 pl.when(g < 2)(lambda: own_to_y(1, odd + 3))
-                to_sib(1, Y, odd)
                 to_sib(1, Z, odd)
 
             @pl.when((j > 0) & (q == 1))
@@ -477,6 +508,7 @@
         keep.start()
         lax.fori_loop(NJ - LAG, last, drain, 0)
         keep.wait()
+        settle()
         for j in (last, last - 1):
             for b in range(2):
                 partial_out(theirs, j, b).wait_send()
@@ -485,22 +517,6 @@
             partial_out(theirs, last, b).wait_recv()
 
     pl.run_scoped(both, pltpu.VMEM((SLOTS, ROWS, W), jnp.float32))
-
-    for u in range(2):
-        diag_half(u).wait_send()
-    for i in range(nx):
-        xn_send(i).wait_send()
-
-    def sent(c, _):
-        for w in range(2):
-            for kind in range(7):
-                if w == 0 and kind == 6:
-                    pl.when(c < NC - 1)(lambda: copy(0, 6, Y, Y, c, to_y).wait_send())
-                else:
-                    copy(w, kind, Y, Y, c, to_y).wait_send()
-        return _
-
-    lax.fori_loop(0, NC, sent, 0)
 
 
 def _finish(at, x, o, r, y, out, rows, xv, ov, rv, small, came, went):
@@ -562,8 +578,8 @@
                 pltpu.SemaphoreType.DMA((ROWS // XR,)),
                 pltpu.SemaphoreType.DMA((NJ, 2)),
                 pltpu.SemaphoreType.DMA((NJ, 2)),
-                pltpu.SemaphoreType.DMA((2,)),
-                pltpu.SemaphoreType.DMA((2,)),
+                pltpu.SemaphoreType.DMA((4,)),
+                pltpu.SemaphoreType.DMA((4,)),
                 pltpu.SemaphoreType.DMA((12,)),
             ],
             compiler_params=pltpu.CompilerParams(
@@ -572,7 +588,7 @@
             cost_estimate=pl.CostEstimate(flops=275_000_000_000, bytes_accessed=400_000_000, transcendentals=16_777_216),
         )(x, gamma.reshape(1, D), w1, w2)
         at = lax.rem(lax.axis_index("fsdp") + 1, 2) * HALF + HALF - W
-        blocks = 8
+        blocks = 16
         return pl.pallas_call(
             _finish,
             out_shape=bf16((ROWS, D)),

time: 677 us -> 677 us (level)
  no operation moved by 1% of the time
where the time goes in v5:
time: 677 us; the launch traced here: 676 us
  Pallas kernels  676 us (100%)
    pallas_call x1, Pallas kernels, body(): pl.pallas_call(_kernel, out_shape=[bf16((ROWS, D)), jax.ShapeDtypeStruct(...  669 us

profile of v5, /device:TPU:0, one launch (start us, length us, event | category | flops | bytes accessed | tf_op | source)
XLA Modules:
  0.0 676.3 jit_solution(14372292776562294244)
XLA Ops:
  0.0 668.5 %shard_map.46 = (bf16[1024,4096]{1,0:T(8,128)(2,1)}, f32[1024,256]{1,0:T(8,128)}, bf16[8,8,2048,256]{3,2,1,0:T(8,128)(2,1)}, bf16[8,8,2048,256]{3,2,1,0:T(8,128)...) custom-call(bf16[1024,4096]{1,0:T(8,128)(2,1)} %x.3, f32[1,4096]{1,0:T(1,128)} %bitcast.2, ...), custom_call_target="tpu_custom_call" | custom-call | flops 275000000512 | bytes 400000000 | tf_op jit(solution)/shard_map/pallas_call | solution.py:559
  668.5 7.6 %shard_map.47 = bf16[1024,4096]{1,0:T(8,128)(2,1)} custom-call(s32[1]{0:T(128)} %bitcast.at, bf16[1024,4096]{1,0:T(8,128)(2,1)} %x.3, f32[1024,256]{1,0:T(8,128)} %get-tuple-element.8.o, f32[16,1024,256]{2,1,0:T(8,128)} %get-tuple-element.9.r, bf16[1024,4096]{1,0:T(8,128)(2,1)} %get-tuple-element.10.y), custom_call_target="tpu_custom_call" | custom-call | tf_op jit(solution)/shard_map/pallas_call | solution.py:592
